TPU v7x, 32 devices: a whole 2x2x4 slice. The times are simulated.
32 devices in a mesh: mem: 4 (over x, core), lat: 8 (over z, y).
Axes of the slice: x: 2, y: 2, z: 4, core: 2. Of those that a mesh axis runs over, the one named last changes fastest.
Arguments:
- control: bfloat16 [8, 10, 704, 1440], P('mem', None, 'lat'), may hold values from -6 to 6
- perturb: bfloat16 [8, 10, 704, 1440], P('mem', None, None, 'lat'), may hold values from -6 to 6
- lon_loc: bfloat16 [1440, 1440], P(None, 'mem'), may hold values from 0 to 1, as said below
- lat_loc: bfloat16 [704, 704], P('mem'), may hold values from 0 to 1, as said below
- static_scale: float32 [10, 704, 1440], P(None, 'mem', 'lat'), may hold values from 0.3 to 1
- static_field: float32 [10, 704, 1440], P(None, 'mem', 'lat'), may hold values from -6 to 6
- courant: float32 [2, 704, 1440], P(None, 'mem', 'lat'), may hold values from -0.48 to 0.48
Outputs:
- increment: float32 [10, 704, 1440], P(None, 'mem', 'lat')
- evolved: float32 [10, 704, 1440], P(None, 'mem', 'lat')
Inputs may be any that keep to these rules, and one draw needn't show every extreme that they name: `lon_loc`: Symmetric, with positive entries. `lat_loc`: Symmetric, with positive entries.
All inputs are finite; a program needn't handle non-finite values.
Results may differ from a plain program's by a relative error of at most 0.0027.
Values may be sent and summed in bfloat16 or wider, within the bound.
No kernel may reach another device: no remote copies, remote signals or barrier semaphores. Data moves between devices by JAX's collectives and lax.ppermute only.
A program may use at most 128 MiB of HBM per device.

v0:
```python
import math
import jax
import jax.numpy as jnp
from jax import lax
from jax.sharding import PartitionSpec as P

NLAT = 704
STEPS = 4


def padded_2(shard, sides, width, wrap):
    for axis, dim in sides:
        size, length = (lax.axis_size(axis), shard.shape[dim])
        up = [(i, (i + 1) % size) for i in range(size if wrap else size - 1)]
        down = [(j, i) for i, j in up]
        last = lax.slice_in_dim(shard, length - width, length, axis=dim)
        leading = lax.slice_in_dim(shard, 0, width, axis=dim)
        before = lax.ppermute(last, axis, up)
        after = lax.ppermute(leading, axis, down)
        shard = jnp.concatenate([before, shard, after], axis=dim)
    return shard


def upwind(padded, east_west, north_south):
    center = padded[:, 1:-1, 1:-1]
    western = padded[:, 1:-1, :-2]
    eastern = padded[:, 1:-1, 2:]
    southern = padded[:, :-2, 1:-1]
    northern = padded[:, 2:, 1:-1]
    zonal = jnp.maximum(east_west, 0.0) * (center - western) + jnp.minimum(east_west, 0.0) * (
        eastern - center
    )
    meridional = jnp.maximum(north_south, 0.0) * (center - southern) + jnp.minimum(
        north_south, 0.0
    ) * (northern - center)
    return center - zonal - meridional


def lon_rim(values, width):
    return padded_2(values, (("lat", 2),), width, True)


def lat_rim(values, width):
    return padded_2(values, (("mem", 1),), width, False)


def evolve(current, courant):
    fields = current.shape[0]
    stacked = jnp.concatenate([current, courant], axis=0)
    extended = lat_rim(lon_rim(stacked, STEPS), STEPS)
    result = extended[:fields]
    wind_ext = extended[fields:]
    for step_index in range(STEPS):
        margin = step_index + 1
        inner_wind = wind_ext[
            :, margin : wind_ext.shape[1] - margin, margin : wind_ext.shape[2] - margin
        ]
        result = upwind(result, inner_wind[0], inner_wind[1])
    return result


def per_device(control, perturb, lon_loc, lat_loc, static_scale, static_field, courant):
    along_lon = jnp.einsum(
        "mfal,lc->amfc",
        control,
        lax.all_gather(lon_loc, "mem", axis=1, tiled=True),
        preferred_element_type=jnp.float32,
    ).astype(jnp.bfloat16)
    banded = lax.all_to_all(along_lon, "lat", split_axis=3, concat_axis=0, tiled=True)
    mem_here = banded.shape[1]
    fields = banded.shape[2]
    lon_width = banded.shape[3]
    flat_band = banded.reshape(banded.shape[0], mem_here * fields * lon_width)
    pert_rows = jnp.transpose(perturb, (2, 0, 1, 3))
    lat_weights_all = lax.all_gather(lat_loc, "mem", axis=0, tiled=True)
    members = mem_here * lax.axis_size("mem")
    ens_scale = 1.0 / math.sqrt(members - 1)
    rows_own = NLAT // lax.axis_size("mem")
    localized = jnp.dot(lat_weights_all, flat_band, preferred_element_type=jnp.float32)
    localized = localized.reshape(NLAT, mem_here, fields, lon_width)
    ensemble_all = jnp.transpose(
        lax.psum(jnp.sum(localized * pert_rows.astype(jnp.float32), axis=1) * ens_scale, "mem"),
        (1, 0, 2),
    )
    offset = lax.axis_index("mem") * rows_own
    ensemble = lax.dynamic_slice_in_dim(ensemble_all, offset, rows_own, 1)
    increment = ensemble + static_scale * static_field
    evolved = evolve(increment, courant)
    return (increment, evolved)


def solution(mesh):
    placed = (
        P("mem", None, "lat", None),
        P("mem", None, None, "lat"),
        P(None, "mem"),
        P("mem", None),
        P(None, "mem", "lat"),
        P(None, "mem", "lat"),
        P(None, "mem", "lat"),
    )
    return jax.shard_map(
        per_device,
        mesh=mesh,
        in_specs=placed,
        out_specs=(P(None, "mem", "lat"), P(None, "mem", "lat")),
        check_vma=False,
    )
```

profile of v0, /device:TPU:1, one launch (start us, length us, event | category | flops | bytes accessed | tf_op | source)
XLA Modules:
  0.0 472.6 jit_solution(8537434043374464706)
XLA Ops:
  7.2 0.0 all-gather.2.cloned.1.call-start
  7.2 2.4 copy.32
  9.6 38.8 %all-gather.2.cloned.1.call-done = bf16[1440,1440]{0,1:T(8,128)(2,1)} async-done(((bf16[1440,360]{0,1:T(8,128)(2,1)}), bf16[1440,1440]{0,1:T(8,128)(2,1)}) %all-gather.2.cloned.1.call-update) | async-done | bytes 4147216 | tf_op jit(solution)/shard_map/all_gather | solution.py:66
  48.4 13.5 %convert_bitcast_fusion = bf16[88,2,10,1440]{3,0,2,1:T(8,128)(2,1)} fusion(bf16[2,10,88,1440]{3,2,1,0:T(8,128)(2,1)} %param.7, bf16[1440,1440]{0,1:T(8,128)(2,1)} %all-gather.2.cloned.1.call-done), kind=kOutput, calls=%fused_computation.4 | convolution fusion | flops 7301606400 | bytes 14284800 | tf_op jit(solution)/shard_map/mfal,lc->amfc/dot_general | solution.py:63
  61.8 16.8 %copy.34 = bf16[88,2,10,1440]{0,1,2,3:T(2,128)(2,1)} copy(bf16[88,2,10,1440]{3,0,2,1:T(8,128)(2,1)} %convert_bitcast_fusion) | data formatting | bytes 10137600 | tf_op jit(solution)/shard_map/convert_element_type | solution.py:68
  78.6 5.4 %all-to-all-start = ((bf16[88,2,10,1440]{0,1,2,3:T(2,128)(2,1)}), bf16[88,2,10,1440]{0,1,2,3:T(2,128)(2,1)}, u32[]{:S(2)}, u32[]{:S(2)}) async-start(bf16[88,2,10,1440]{0,1,2,3:T(2,128)(2,1)} %copy.34), calls=%async_computation | async-start | bytes 14745600 | tf_op jit(solution)/shard_map/all_to_all | solution.py:69
  84.0 10.5 %all_gather.7 = bf16[704,704]{1,0:T(8,128)(2,1)S(1)} all-gather(bf16[176,704]{1,0:T(8,128)(2,1)S(1)} %copy-done.7), channel_id=1, replica_groups=mesh['mem'=4,'lat'=8] {'mem'}, dimensions={0}, use_global_device_ids=true | all-gather | bytes 1239040 | tf_op jit(solution)/shard_map/all_gather | solution.py:75
  94.5 150.4 %all-to-all-done = bf16[88,2,10,1440]{0,1,2,3:T(2,128)(2,1)} async-done(((bf16[88,2,10,1440]{0,1,2,3:T(2,128)(2,1)}), bf16[88,2,10,1440]{0,1,2,3:T(2,128)(2,1)}, u32[]{:S(2)}, u32[]{:S(2)}) %all-to-all-start) | async-done | bytes 5068832 | tf_op jit(solution)/shard_map/all_to_all | solution.py:69
  245.0 8.0 %copy.59 = bf16[88,2,10,8,180]{0,3,4,2,1:T(8,128)(2,1)} copy(bf16[88,2,10,8,180]{0,1,2,4,3:T(2,128)(2,1)} %bitcast.2) | data formatting | bytes 10137600 | tf_op jit(solution)/shard_map/all_to_all | solution.py:69
  253.0 12.2 %reshape.11 = bf16[704,3600]{0,1:T(8,128)(2,1)} reshape(bf16[8,88,2,10,180]{1,0,4,3,2:T(8,128)(2,1)} %bitcast.58) | data formatting | bytes 10137600 | tf_op jit(solution)/shard_map/reshape | solution.py:73
  265.2 9.6 %convolution_bitcast_fusion = f32[704,3600]{1,0:T(8,128)} fusion(bf16[704,3600]{0,1:T(8,128)(2,1)} %reshape.11, bf16[704,704]{1,0:T(8,128)(2,1)S(1)} %all_gather.7), kind=kOutput, calls=%fused_computation.3 | convolution fusion | flops 3568435200 | bytes 16197632 | tf_op jit(solution)/shard_map/dot_general | solution.py:79
  274.7 11.8 %copy.36 = f32[704,3600]{0,1:T(8,128)} copy(f32[704,3600]{1,0:T(8,128)} %convolution_bitcast_fusion) | data formatting | bytes 20275200 | tf_op jit(solution)/shard_map/dot_general | solution.py:79
  286.6 11.6 %reshape.12 = f32[704,2,10,180]{0,3,2,1:T(8,128)} reshape(f32[704,3600]{0,1:T(8,128)} %copy.36) | data formatting | bytes 20275200 | tf_op jit(solution)/shard_map/reshape | solution.py:80
  298.1 10.3 %fusion = f32[704,10,180]{0,2,1:T(8,128)} fusion(f32[704,2,10,180]{0,3,2,1:T(8,128)} %reshape.12, bf16[2,10,704,180]{2,0,3,1:T(2,128)(2,1)} %param.8), kind=kLoop, calls=%fused_computation.1 | loop fusion | flops 6336000 | bytes 20275200 | tf_op jit(solution)/shard_map/reduce_sum | solution.py:82
  308.4 5.5 %broadcast_multiply_fusion = f32[704,10,180]{0,2,1:T(8,128)} fusion(f32[704,10,180]{0,2,1:T(8,128)} %fusion), kind=kLoop, calls=%fused_computation.6 | loop fusion | flops 1267200 | bytes 10137600 | tf_op jit(solution)/shard_map/mul | solution.py:82
  314.0 1.5 copy-done.1
  315.4 1.8 copy.38
  317.3 3.0 copy.39
  320.3 0.2 copy.40
  320.5 101.5 %all-reduce.2.cloned.1.call-done = f32[704,10,180]{0,2,1:T(8,128)} async-done(((f32[704,10,180]{0,2,1:T(8,128)}), f32[704,10,180]{0,2,1:T(8,128)}) %all-reduce.2.cloned.1.call-update) | async-done | bytes 5068816 | tf_op jit(solution)/shard_map/psum | solution.py:82
  422.0 3.5 bitcast_add_fusion
  425.6 1.2 collective-permute-start
  426.8 3.0 collective-permute-start.1
  429.8 1.6 collective-permute-done
  431.6 0.3 pad_maximum_fusion
  431.8 1.4 fusion.34
  433.2 2.4 copy.45
  435.6 4.1 collective-permute-start.2
  439.7 1.1 copy.46
  440.8 2.1 collective-permute-start.3
  443.0 1.1 maximum_bitcast_fusion.7
  444.0 0.8 copy.49
  444.8 0.8 copy.50
  445.6 0.8 copy.51
  446.4 0.8 copy.52
  447.2 1.8 copy.53
  449.0 1.2 copy.47
  450.3 2.2 copy.48
  452.5 1.3 maximum_bitcast_fusion.3
  453.8 0.0 copy-done
  453.9 0.3 maximum_bitcast_fusion.5
  454.1 0.3 maximum_bitcast_fusion.1
  454.4 1.0 pad_maximum_fusion.1
  455.6 2.1 fusion.4
  457.7 2.0 fusion.28
  459.8 2.0 fusion.20
  461.8 2.1 fusion.12
  463.9 1.8 copy.54
  (28 shorter events, 0.3 us)
Async XLA Ops:
  7.2 41.2 %all-gather.2.cloned.1.call-start = ((), (), s32[]{:S(2)}) async-start(), calls=%async_computation.1 | async-start | bytes 5529600 | tf_op jit(solution)/shard_map/all_gather | solution.py:66
  78.6 5.4 %copy-start.7 = (bf16[176,704]{1,0:T(8,128)(2,1)S(1)}, bf16[176,704]{1,0:T(8,128)(2,1)}, u32[]{:S(2)}) copy-start(bf16[176,704]{1,0:T(8,128)(2,1)} %param.10) | copy-start | bytes 743428
  78.6 166.4 %all-to-all-start = ((bf16[88,2,10,1440]{0,1,2,3:T(2,128)(2,1)}), bf16[88,2,10,1440]{0,1,2,3:T(2,128)(2,1)}, u32[]{:S(2)}, u32[]{:S(2)}) async-start(bf16[88,2,10,1440]{0,1,2,3:T(2,128)(2,1)} %copy.34), calls=%async_computation | async-start | bytes 14745600 | tf_op jit(solution)/shard_map/all_to_all | solution.py:69
  84.0 338.0 %all-reduce.2.cloned.1.call-start = ((), (), s32[]{:S(2)}) async-start(), calls=%async_computation.2 | async-start | bytes 11304960 | tf_op jit(solution)/shard_map/psum | solution.py:82
  313.9 1.5 copy-start.1
  317.3 3.0 copy-start.2
  425.6 5.9 %collective-permute-start = (f32[12,176,4]{1,0,2:T(8,128)S(1)}, f32[12,176,4]{1,0,2:T(8,128)S(1)}, u32[]{:S(2)}, u32[]{:S(2)}) collective-permute-start(f32[12,176,4]{1,0,2:T(8,128)S(1)} %copy.41), channel_id=1, source_target_pairs={{0,1},{1,2},{2,3},{3,4},{4,5},{5,6},{6,7},{7,0},{8,9},{9,10},{10,1... | collective-permute-start | bytes 101384 | tf_op jit(solution)/shard_map/ppermute | solution.py:18
  426.8 4.7 collective-permute-start.1
  435.6 13.4 %collective-permute-start.2 = (f32[12,4,188]{2,1,0:T(4,128)}, f32[12,4,188]{2,1,0:T(4,128)}, u32[]{:S(2)}, u32[]{:S(2)}) collective-permute-start(f32[12,4,188]{2,1,0:T(4,128)} %copy.45), channel_id=1, source_target_pairs={{0,8},{8,16},{16,24},{1,9},{9,17},{17,25},{2,10},{10,18},{18,26},{... | collective-permute-start | bytes 108296 | tf_op jit(solution)/shard_map/ppermute | solution.py:18
  440.8 9.4 %collective-permute-start.3 = (f32[12,4,188]{2,1,0:T(4,128)}, f32[12,4,188]{2,1,0:T(4,128)}, u32[]{:S(2)}, u32[]{:S(2)}) collective-permute-start(f32[12,4,188]{2,1,0:T(4,128)} %copy.46), channel_id=1, source_target_pairs={{8,0},{16,8},{24,16},{9,1},{17,9},{25,17},{10,2},{18,10},{26,18},{... | collective-permute-start | bytes 108296 | tf_op jit(solution)/shard_map/ppermute | solution.py:19
  452.5 1.4 copy-start
  459.7 2.1 copy-start.3
  459.7 2.1 copy-start.4
  459.7 2.1 copy-start.5
  459.7 2.1 copy-start.6
Sparse Core Ops, SparseCore 0:
  10.1 38.2 all-gather.1
  314.1 107.8 all-reduce.1
where the time goes:
time: 474 us; the launch traced here: 473 us
  waiting for transfers between devices  292 us (62%)
  local copies, waits for them, and re-layouts  84.6 us (18%)
  other arithmetic  31.8 us (7%)
  matrix products  23 us (5%)
  starting transfers between devices  16 us (3%)
  between operations  14.3 us (3%)
  blocking collectives  10.5 us (2%)
    all_to_all x1, waiting for transfers between devices, per_device(): lax.all_to_all(along_lon, 'lat', split_axis=3, concat_axis=0, tiled=True)  150 us
    psum x1, waiting for transfers between devices, per_device(): lax.psum(jnp.sum(localized * pert_rows.astype(jnp.float32), axis=1) * ens...  102 us
    all_gather x1, waiting for transfers between devices, per_device(): lax.all_gather(lon_loc, 'mem', axis=1, tiled=True)  38.8 us
    convert_element_type x1, local copies, waits for them, and re-layouts, per_device(): along_lon = jnp.einsum('mfal,lc->amfc', control, lax.all_gather(lon_loc,...  16.8 us
    dot_general x1, matrix products, per_device(): jnp.einsum('mfal,lc->amfc', control, lax.all_gather(lon_loc, 'mem', axis=...  13.5 us
    unnamed x22, local copies, waits for them, and re-layouts  12.6 us
    reshape x1, local copies, waits for them, and re-layouts, per_device(): flat_band = banded.reshape(banded.shape[0], mem_here * fields * lon_width)  12.2 us
    dot_general x1, local copies, waits for them, and re-layouts, per_device(): jnp.dot(lat_weights_all, flat_band, preferred_element_type=jnp.float32)  11.8 us
  transfers between devices with their start and end apart: 7, of which 4 were waited for; matrix products, arithmetic and copies ran while one was open for 3% of the time, Pallas kernels for 0%

commit v1 on v0

--- a/solution.py
+++ b/solution.py
@@ -63,7 +63,9 @@
     along_lon = jnp.einsum(
         "mfal,lc->amfc",
         control,
-        lax.all_gather(lon_loc, "mem", axis=1, tiled=True),
+        jnp.concatenate(
+            lax.all_to_all(jnp.stack([lon_loc] * lax.axis_size("mem")), "mem", 0, 0), 1
+        ),
         preferred_element_type=jnp.float32,
     ).astype(jnp.bfloat16)
     banded = lax.all_to_all(along_lon, "lat", split_axis=3, concat_axis=0, tiled=True)

time: 474 us -> 510 us (1.076)
  blocking collectives: 10.5 us -> 64.2 us
  waiting for transfers between devices: 292 us -> 254 us
  local copies, waits for them, and re-layouts: 84.6 us -> 105 us
    all_to_all x0 -> x1, blocking collectives: none -> 53.7 us  [per_device(): lax.all_to_all(jnp.stack([lon_loc] * lax.axis_size('mem')), 'mem', 0, 0)]
    all_gather x1 -> x0, waiting for transfers between devices: 38.8 us -> none  [per_device(): lax.all_gather(lon_loc, 'mem', axis=1, tiled=True)]
    reshape x0 -> x2, local copies, waits for them, and re-layouts: none -> 20.7 us  [per_device(): jnp.concatenate(lax.all_to_all(jnp.stack([lon_loc] * lax.axis_size('mem')...]
    unnamed x22 -> x21, local copies, waits for them, and re-layouts: 12.6 us -> 10.3 us
  transfers between devices with their start and end apart: 7 -> 6, of which waited for: 4 -> 3; matrix products, arithmetic and copies ran while one was open for 3% -> 3% of each run, Pallas kernels for 0% -> 0%
where the time goes in v1:
time: 510 us; the launch traced here: 508 us
  waiting for transfers between devices  254 us (50%)
  local copies, waits for them, and re-layouts  105 us (21%)
  blocking collectives  64.2 us (13%)
  other arithmetic  31.8 us (6%)
  matrix products  22.9 us (4%)
  starting transfers between devices  16.2 us (3%)
  between operations  14.3 us (3%)
    all_to_all x1, waiting for transfers between devices, per_device(): lax.all_to_all(along_lon, 'lat', split_axis=3, concat_axis=0, tiled=True)  150 us
    psum x1, waiting for transfers between devices, per_device(): lax.psum(jnp.sum(localized * pert_rows.astype(jnp.float32), axis=1) * ens...  102 us
    all_to_all x1, blocking collectives, per_device(): lax.all_to_all(jnp.stack([lon_loc] * lax.axis_size('mem')), 'mem', 0, 0)  53.7 us
    reshape x2, local copies, waits for them, and re-layouts, per_device(): jnp.concatenate(lax.all_to_all(jnp.stack([lon_loc] * lax.axis_size('mem')...  20.7 us
    convert_element_type x1, local copies, waits for them, and re-layouts, per_device(): along_lon = jnp.einsum('mfal,lc->amfc', control, jnp.concatenate(lax.all_...  16.8 us
    dot_general x1, matrix products, per_device(): jnp.einsum('mfal,lc->amfc', control, jnp.concatenate(lax.all_to_all(jnp.s...  13.4 us
    reshape x1, local copies, waits for them, and re-layouts, per_device(): flat_band = banded.reshape(banded.shape[0], mem_here * fields * lon_width)  12.2 us
    dot_general x1, local copies, waits for them, and re-layouts, per_device(): jnp.dot(lat_weights_all, flat_band, preferred_element_type=jnp.float32)  11.8 us
  transfers between devices with their start and end apart: 6, of which 3 were waited for; matrix products, arithmetic and copies ran while one was open for 3% of the time, Pallas kernels for 0%

profile of v1, /device:TPU:1, one launch (start us, length us, event | category | flops | bytes accessed | tf_op | source)
XLA Modules:
  0.0 508.0 jit_solution(11755760181248296988)
XLA Ops:
  7.2 1.6 stack.2
  8.8 53.7 %all_to_all.20 = bf16[4,1440,360]{2,1,0:T(8,128)(2,1)S(1)} all-to-all(bf16[4,1440,360]{2,1,0:T(8,128)(2,1)S(1)} %stack.2), channel_id=1, replica_groups=mesh['mem'=4,'lat'=8] {'mem'}, dimensions={0} | all-to-all | bytes 8294400 | tf_op jit(solution)/shard_map/all_to_all | solution.py:67
  62.5 12.0 %copy.31 = bf16[1440,4,360]{2,1,0:T(4,128)(2,1)} copy(bf16[1440,4,360]{2,0,1:T(8,128)(2,1)S(1)} %bitcast.60) | data formatting | bytes 8294400 | tf_op jit(solution)/shard_map/reshape | solution.py:66
  74.5 8.7 %reshape.23 = bf16[1440,1440,1,1]{1,0,2,3:T(8,128)(2,1)} reshape(bf16[1440,4,360]{2,1,0:T(4,128)(2,1)} %copy.31) | data formatting | bytes 8294400 | tf_op jit(solution)/shard_map/reshape | solution.py:66
  83.2 13.4 %convert_bitcast_fusion = bf16[88,2,10,1440]{3,0,2,1:T(8,128)(2,1)} fusion(bf16[2,10,88,1440]{3,2,1,0:T(8,128)(2,1)} %param.7, bf16[1440,1440,1,1]{1,0,2,3:T(8,128)(2,1)} %reshape.23), kind=kOutput, calls=%fused_computation.4 | convolution fusion | flops 7301606400 | bytes 14284800 | tf_op jit(solution)/shard_map/mfal,lc->amfc/dot_general | solution.py:63
  96.6 16.8 %copy.32 = bf16[88,2,10,1440]{0,1,2,3:T(2,128)(2,1)} copy(bf16[88,2,10,1440]{3,0,2,1:T(8,128)(2,1)} %convert_bitcast_fusion) | data formatting | bytes 10137600 | tf_op jit(solution)/shard_map/convert_element_type | solution.py:70
  113.4 5.7 %all-to-all-start.1 = ((bf16[88,2,10,1440]{0,1,2,3:T(2,128)(2,1)}), bf16[88,2,10,1440]{0,1,2,3:T(2,128)(2,1)}, u32[]{:S(2)}, u32[]{:S(2)}) async-start(bf16[88,2,10,1440]{0,1,2,3:T(2,128)(2,1)} %copy.32), calls=%async_computation.1 | async-start | bytes 14745600 | tf_op jit(solution)/shard_map/all_to_all | solution.py:71
  119.2 10.5 %all_gather.3 = bf16[704,704]{1,0:T(8,128)(2,1)S(1)} all-gather(bf16[176,704]{1,0:T(8,128)(2,1)S(1)} %copy-done.7), channel_id=1, replica_groups=mesh['mem'=4,'lat'=8] {'mem'}, dimensions={0}, use_global_device_ids=true | all-gather | bytes 1239040 | tf_op jit(solution)/shard_map/all_gather | solution.py:77
  129.7 149.8 %all-to-all-done.1 = bf16[88,2,10,1440]{0,1,2,3:T(2,128)(2,1)} async-done(((bf16[88,2,10,1440]{0,1,2,3:T(2,128)(2,1)}), bf16[88,2,10,1440]{0,1,2,3:T(2,128)(2,1)}, u32[]{:S(2)}, u32[]{:S(2)}) %all-to-all-start.1) | async-done | bytes 5068832 | tf_op jit(solution)/shard_map/all_to_all | solution.py:71
  279.5 8.0 %copy.56 = bf16[88,2,10,8,180]{0,3,4,2,1:T(8,128)(2,1)} copy(bf16[88,2,10,8,180]{0,1,2,4,3:T(2,128)(2,1)} %bitcast.3) | data formatting | bytes 10137600 | tf_op jit(solution)/shard_map/all_to_all | solution.py:71
  287.5 12.2 %reshape.21 = bf16[704,3600]{0,1:T(8,128)(2,1)} reshape(bf16[8,88,2,10,180]{1,0,4,3,2:T(8,128)(2,1)} %bitcast.59) | data formatting | bytes 10137600 | tf_op jit(solution)/shard_map/reshape | solution.py:75
  299.7 9.5 %convolution_bitcast_fusion = f32[704,3600]{1,0:T(8,128)} fusion(bf16[704,3600]{0,1:T(8,128)(2,1)} %reshape.21, bf16[704,704]{1,0:T(8,128)(2,1)S(1)} %all_gather.3), kind=kOutput, calls=%fused_computation.3 | convolution fusion | flops 3568435200 | bytes 16197632 | tf_op jit(solution)/shard_map/dot_general | solution.py:81
  309.2 11.8 %copy.34 = f32[704,3600]{0,1:T(8,128)} copy(f32[704,3600]{1,0:T(8,128)} %convolution_bitcast_fusion) | data formatting | bytes 20275200 | tf_op jit(solution)/shard_map/dot_general | solution.py:81
  321.1 11.6 %reshape.22 = f32[704,2,10,180]{0,3,2,1:T(8,128)} reshape(f32[704,3600]{0,1:T(8,128)} %copy.34) | data formatting | bytes 20275200 | tf_op jit(solution)/shard_map/reshape | solution.py:82
  332.7 10.3 %fusion = f32[704,10,180]{0,2,1:T(8,128)} fusion(f32[704,2,10,180]{0,3,2,1:T(8,128)} %reshape.22, bf16[2,10,704,180]{2,0,3,1:T(2,128)(2,1)} %param.8), kind=kLoop, calls=%fused_computation.1 | loop fusion | flops 6336000 | bytes 20275200 | tf_op jit(solution)/shard_map/reduce_sum | solution.py:84
  343.0 5.5 %broadcast_multiply_fusion = f32[704,10,180]{0,2,1:T(8,128)} fusion(f32[704,10,180]{0,2,1:T(8,128)} %fusion), kind=kLoop, calls=%fused_computation.6 | loop fusion | flops 1267200 | bytes 10137600 | tf_op jit(solution)/shard_map/mul | solution.py:84
  348.5 1.5 copy-done.1
  350.0 1.8 copy.36
  351.8 3.0 copy.37
  354.8 0.2 copy.38
  355.0 102.3 %all-reduce.2.cloned.1.call-done = f32[704,10,180]{0,2,1:T(8,128)} async-done(((f32[704,10,180]{0,2,1:T(8,128)}), f32[704,10,180]{0,2,1:T(8,128)}) %all-reduce.2.cloned.1.call-update) | async-done | bytes 5068816 | tf_op jit(solution)/shard_map/psum | solution.py:84
  457.3 3.5 bitcast_add_fusion
  460.9 1.2 collective-permute-start
  462.1 3.0 collective-permute-start.1
  465.2 1.6 collective-permute-done
  466.9 0.3 pad_maximum_fusion
  467.1 1.4 fusion.34
  468.6 2.4 copy.43
  470.9 4.1 collective-permute-start.2
  475.1 1.1 copy.44
  476.2 2.1 collective-permute-start.3
  478.3 1.1 maximum_bitcast_fusion.7
  479.4 0.8 copy.47
  480.2 0.8 copy.48
  480.9 0.8 copy.49
  481.7 0.8 copy.50
  482.5 1.8 copy.51
  484.4 1.2 copy.45
  485.6 2.2 copy.46
  487.8 1.3 maximum_bitcast_fusion.3
  489.2 0.3 maximum_bitcast_fusion.5
  489.5 0.3 maximum_bitcast_fusion.1
  489.8 1.0 pad_maximum_fusion.1
  490.9 2.1 fusion.4
  493.0 2.0 fusion.28
  495.1 2.1 fusion.20
  497.2 2.1 fusion.12
  499.3 1.8 copy.52
  (28 shorter events, 0.3 us)
Async XLA Ops:
  113.4 5.7 %copy-start.7 = (bf16[176,704]{1,0:T(8,128)(2,1)S(1)}, bf16[176,704]{1,0:T(8,128)(2,1)}, u32[]{:S(2)}) copy-start(bf16[176,704]{1,0:T(8,128)(2,1)} %param.10) | copy-start | bytes 743428
  113.4 166.0 %all-to-all-start.1 = ((bf16[88,2,10,1440]{0,1,2,3:T(2,128)(2,1)}), bf16[88,2,10,1440]{0,1,2,3:T(2,128)(2,1)}, u32[]{:S(2)}, u32[]{:S(2)}) async-start(bf16[88,2,10,1440]{0,1,2,3:T(2,128)(2,1)} %copy.32), calls=%async_computation.1 | async-start | bytes 14745600 | tf_op jit(solution)/shard_map/all_to_all | solution.py:71
  119.1 338.2 %all-reduce.2.cloned.1.call-start = ((), (), s32[]{:S(2)}) async-start(), calls=%async_computation.2 | async-start | bytes 11304960 | tf_op jit(solution)/shard_map/psum | solution.py:84
  348.5 1.5 copy-start.1
  351.8 3.0 copy-start.2
  460.9 5.9 %collective-permute-start = (f32[12,176,4]{1,0,2:T(8,128)S(1)}, f32[12,176,4]{1,0,2:T(8,128)S(1)}, u32[]{:S(2)}, u32[]{:S(2)}) collective-permute-start(f32[12,176,4]{1,0,2:T(8,128)S(1)} %copy.39), channel_id=1, source_target_pairs={{0,1},{1,2},{2,3},{3,4},{4,5},{5,6},{6,7},{7,0},{8,9},{9,10},{10,1... | collective-permute-start | bytes 101384 | tf_op jit(solution)/shard_map/ppermute | solution.py:18
  462.1 4.7 collective-permute-start.1
  470.9 13.4 %collective-permute-start.2 = (f32[12,4,188]{2,1,0:T(4,128)}, f32[12,4,188]{2,1,0:T(4,128)}, u32[]{:S(2)}, u32[]{:S(2)}) collective-permute-start(f32[12,4,188]{2,1,0:T(4,128)} %copy.43), channel_id=1, source_target_pairs={{0,8},{8,16},{16,24},{1,9},{9,17},{17,25},{2,10},{10,18},{18,26},{... | collective-permute-start | bytes 108296 | tf_op jit(solution)/shard_map/ppermute | solution.py:18
  476.2 9.4 %collective-permute-start.3 = (f32[12,4,188]{2,1,0:T(4,128)}, f32[12,4,188]{2,1,0:T(4,128)}, u32[]{:S(2)}, u32[]{:S(2)}) collective-permute-start(f32[12,4,188]{2,1,0:T(4,128)} %copy.44), channel_id=1, source_target_pairs={{8,0},{16,8},{24,16},{9,1},{17,9},{25,17},{10,2},{18,10},{26,18},{... | collective-permute-start | bytes 108296 | tf_op jit(solution)/shard_map/ppermute | solution.py:19
  487.8 1.4 copy-start
  495.1 2.1 copy-start.3
  495.1 2.1 copy-start.4
  495.1 2.1 copy-start.5
  495.1 2.1 copy-start.6
Sparse Core Ops, SparseCore 0:
  348.6 108.6 all-reduce.1
